TPU v7x, 16 devices: a whole 2x2x2 slice. The times are simulated.
16 devices in a mesh: pool: 16 (over z, y, x, core).
Axes of the slice: x: 2, y: 2, z: 2, core: 2. Of those that a mesh axis runs over, the one named last changes fastest.
Arguments:
- queries: bfloat16 [64, 128, 40, 128], P('pool')
- k_new: bfloat16 [64, 128, 8, 128], P('pool')
- v_new: bfloat16 [64, 128, 8, 128], P('pool')
- k_pool: bfloat16 [8192, 16, 8, 128], P('pool')
- v_pool: bfloat16 [8192, 16, 8, 128], P('pool')
- block_table: int32 [64, 128], replicated
- write_ids: int32 [64, 8], P('pool')
Outputs:
- output 1: bfloat16 [64, 128, 40, 128], P('pool')
- output 2: bfloat16 [8192, 16, 8, 128], P('pool')
- output 3: bfloat16 [8192, 16, 8, 128], P('pool')
All inputs are finite; a program needn't handle non-finite values.
Results may differ from a plain program's by a relative error of at most 0.00950796.
Values are sent between devices in bfloat16 or wider.
A program may use at most 1 GiB of HBM per device.

v0:
```python
import functools

import jax
import jax.numpy as jnp
from jax import lax
from jax.experimental import pallas as pl
from jax.experimental.pallas import tpu as pltpu
from jax.sharding import PartitionSpec as P

FAST_CAP = 4
FULL_CAP = 20
RELAY_CAP = 2
SHARED_CAP = 8
GROUP = 8
STORE_BLOCKS = 16
GROUP_HEADS = 5
PAIR = 2
CORES = 2
N_CHIPS = 8
EARLY = 3
TILE = 1024
BUF_KEYS = 2048
LIST_PAD = 8
LOG2E = 1.4426950408889634


def gather_kernel(ids_ref, k_hbm, v_hbm, out_ref, buf, sem):
    step, steps = pl.program_id(0), pl.num_programs(0)

    def fetch(at_step, slot):
        for i in range(GROUP):
            block = ids_ref[at_step * GROUP + i]
            pltpu.make_async_copy(k_hbm.at[block], buf.at[slot, i, 0], sem.at[slot]).start()
            pltpu.make_async_copy(v_hbm.at[block], buf.at[slot, i, 1], sem.at[slot]).start()

    @pl.when(step == 0)
    def _():
        fetch(0, 0)

    @pl.when(step + 1 < steps)
    def _():
        fetch(step + 1, (step + 1) % 2)

    slot = step % 2
    pltpu.make_async_copy(buf.at[slot], buf.at[slot], sem.at[slot]).wait()
    heads, block_len, dim = out_ref.shape[2:]
    rows = heads * block_len
    dst = lax.broadcasted_iota(jnp.int32, (rows, rows), 0)
    src = lax.broadcasted_iota(jnp.int32, (rows, rows), 1)
    perm = (src == (dst % block_len) * heads + dst // block_len).astype(jnp.bfloat16)
    for i in range(GROUP):
        pair = jnp.concatenate([buf[slot, i, 0], buf[slot, i, 1]], axis=1)
        moved = jnp.dot(perm, pair, preferred_element_type=jnp.float32).astype(jnp.bfloat16)
        out_ref[i, 0] = moved[:, :dim].reshape(heads, block_len, dim)
        out_ref[i, 1] = moved[:, dim:].reshape(heads, block_len, dim)


def gather_blocks(ids, k_flat, v_flat, heads, block_len):
    count, dim = ids.shape[0], k_flat.shape[-1]
    block = (GROUP, 2, heads, block_len, dim)
    return pl.pallas_call(
        gather_kernel,
        grid_spec=pltpu.PrefetchScalarGridSpec(
            num_scalar_prefetch=1,
            grid=(count // GROUP,),
            in_specs=[pl.BlockSpec(memory_space=pl.ANY)] * 2,
            out_specs=pl.BlockSpec(block, lambda i, ids: (i, 0, 0, 0, 0)),
            scratch_shapes=[
                pltpu.VMEM((2, GROUP, 2, heads * block_len, dim), jnp.bfloat16),
                pltpu.SemaphoreType.DMA((2,)),
            ],
        ),
        out_shape=jax.ShapeDtypeStruct((count,) + block[1:], jnp.bfloat16),
        cost_estimate=pl.CostEstimate(flops=count * 8 * 10 ** 6, bytes_accessed=count * 131072, transcendentals=0),
        name='gather_blocks',
    )(ids, k_flat, v_flat)


def store_kernel(from_ref, k_new_ref, v_new_ref, k_ref, v_ref, k_out, v_out):
    count = k_ref.shape[0]
    for i in range(count):
        new = from_ref[pl.program_id(0) * count + i]

        @pl.when(new < 0)
        def _():
            k_out[i] = k_ref[i]
            v_out[i] = v_ref[i]

        @pl.when(new >= 0)
        def _():
            k_out[i] = k_new_ref[new]
            v_out[i] = v_new_ref[new]


def store_chunk(write_ids, k_new, v_new, k_flat, v_flat):
    blocks, rows, dim = k_flat.shape
    k_new, v_new = k_new.reshape(-1, rows, dim), v_new.reshape(-1, rows, dim)
    targets = write_ids.reshape(-1)
    hit = targets[None, :] == jnp.arange(blocks)[:, None]
    from_new = jnp.sum(jnp.where(hit, jnp.arange(targets.shape[0]) + 1, 0), axis=1) - 1
    whole = pl.BlockSpec(k_new.shape, lambda i, ids: (0, 0, 0))
    part = pl.BlockSpec((STORE_BLOCKS, rows, dim), lambda i, ids: (i, 0, 0))
    return pl.pallas_call(
        store_kernel,
        grid_spec=pltpu.PrefetchScalarGridSpec(
            num_scalar_prefetch=1,
            grid=(blocks // STORE_BLOCKS,),
            in_specs=[whole, whole, part, part],
            out_specs=[part, part],
        ),
        out_shape=[jax.ShapeDtypeStruct(k_flat.shape, k_flat.dtype)] * 2,
        cost_estimate=pl.CostEstimate(flops=10 ** 10, bytes_accessed=8 * k_flat.size, transcendentals=0),
        name='store_chunk',
    )(from_new, k_new, v_new, k_flat, v_flat)


def fetch_list(count, at, codes_ref, src_hbm, k_buf, v_buf, sem):
    block_len = src_hbm.shape[3]

    def fetch(e, carry):
        code = codes_ref[at + e]
        rows = pl.ds(pl.multiple_of(e * block_len, block_len), block_len)
        pltpu.make_async_copy(src_hbm.at[code, 0], k_buf.at[:, rows], sem.at[0]).start()
        pltpu.make_async_copy(src_hbm.at[code, 1], v_buf.at[:, rows], sem.at[1]).start()
        return carry

    def settle(t, carry):
        rows = pl.ds(0, TILE)
        pltpu.make_async_copy(k_buf.at[:, rows], k_buf.at[:, rows], sem.at[0]).wait()
        pltpu.make_async_copy(v_buf.at[:, rows], v_buf.at[:, rows], sem.at[1]).wait()
        return carry

    tiles = pl.cdiv(count * block_len, TILE)
    lax.fori_loop(0, tiles * (TILE // block_len), fetch, 0)
    lax.fori_loop(0, tiles, settle, 0)


def scores(q, keys):
    return lax.dot_general(q, keys, (((1,), (1,)), ((), ())), preferred_element_type=jnp.float32)


def wide_row(x, n):
    return jnp.concatenate([x] * (n // x.shape[1]), axis=1)


def scan_tiles(pair, keys, factor, q, k_buf, v_buf, top_ref, sum_ref, acc_ref):
    def body(t, carry):
        rows = pl.ds(pl.multiple_of(t * TILE, TILE), TILE)
        col = lax.broadcasted_iota(jnp.int32, (1, TILE), 1)
        bias = jnp.where(col < keys - t * TILE, 0.0, -jnp.inf)
        for j in range(PAIR):
            head = pair * PAIR + j
            s = scores(q[j], k_buf[head, rows]) + bias
            old = top_ref[j]
            top = jnp.maximum(old, jnp.max(s, axis=1, keepdims=True))
            shrink = jnp.exp2((old - top) * factor)
            p = jnp.exp2(s * factor - wide_row(top * factor, TILE))
            sum_ref[j] = sum_ref[j] * shrink + jnp.sum(p, axis=1, keepdims=True)
            part = jnp.dot(p.astype(jnp.bfloat16), v_buf[head, rows], preferred_element_type=jnp.float32)
            acc_ref[j] = acc_ref[j] * shrink + part
            top_ref[j] = top
        return carry

    lax.fori_loop(0, pl.cdiv(keys, TILE), body, 0)


def shared_kernel(codes_ref, q_ref, kn_ref, vn_ref, src_hbm, acc_ref, stat_ref, k_buf, v_buf, top_ref, sum_ref, sem):
    count = codes_ref[0]
    pair = pl.program_id(0)

    @pl.when((pair == 0) & (pl.program_id(1) == 0))
    def _():
        fetch_list(count, 1, codes_ref, src_hbm, k_buf, v_buf, sem)

    _, rows, dim = q_ref.shape
    chunk = kn_ref.shape[1]
    factor = dim ** -0.5 * LOG2E
    row = lax.broadcasted_iota(jnp.int32, (rows, chunk), 0) % chunk
    col = lax.broadcasted_iota(jnp.int32, (rows, chunk), 1)
    for j in range(PAIR):
        s = jnp.where(col <= row, scores(q_ref[j], kn_ref[j]), -jnp.inf)
        top = jnp.max(s, axis=1, keepdims=True)
        p = jnp.exp2(s * factor - top * factor)
        top_ref[j] = jnp.broadcast_to(top, (rows, dim))
        sum_ref[j] = jnp.broadcast_to(jnp.sum(p, axis=1, keepdims=True), (rows, dim))
        acc_ref[j] = jnp.dot(p.astype(jnp.bfloat16), vn_ref[j], preferred_element_type=jnp.float32)
    scan_tiles(pair, count * src_hbm.shape[3], factor, q_ref, k_buf, v_buf, top_ref, sum_ref, acc_ref)
    lane = lax.broadcasted_iota(jnp.int32, (rows, dim), 1)
    for j in range(PAIR):
        stat_ref[j] = jnp.where(lane == 0, top_ref[j], sum_ref[j])


def window_kernel(codes_ref, q_ref, acc_in, stat_in, src_hbm, old_ref, out_ref, k_buf, v_buf, top_ref, sum_ref, acc_ref, wide, sem):
    at = pl.program_id(0) * codes_ref.shape[0] // pl.num_programs(0)
    count = codes_ref[at]
    pair = pl.program_id(1)

    @pl.when(pair == 0)
    def _():
        fetch_list(count, at + 1, codes_ref, src_hbm, k_buf, v_buf, sem)

    _, rows, dim = q_ref.shape
    heads = k_buf.shape[0]
    chunk = rows // GROUP_HEADS
    for j in range(PAIR):
        top_ref[j] = jnp.broadcast_to(stat_in[j, :, 0:1], (rows, dim))
        sum_ref[j] = jnp.broadcast_to(stat_in[j, :, 1:2], (rows, dim))
        acc_ref[j] = acc_in[j]
    factor = dim ** -0.5 * LOG2E
    scan_tiles(pair, count * src_hbm.shape[3], factor, q_ref, k_buf, v_buf, top_ref, sum_ref, acc_ref)
    for j in range(PAIR):
        out = acc_ref[j] * (1.0 / sum_ref[j])
        for i in range(GROUP_HEADS):
            at_head = (pair * PAIR + j) * GROUP_HEADS + i
            wide[pl.ds(at_head, chunk, stride=heads * GROUP_HEADS), :] = out[i * chunk:(i + 1) * chunk]

    @pl.when(pair == heads // PAIR - 1)
    def _():
        out_ref[...] = wide[...].astype(jnp.bfloat16)


def attend_shared(codes, q_t, kn_t, vn_t, source):
    count, heads, rows, dim = q_t.shape
    chunk = kn_t.shape[2]
    part = lambda n: pl.BlockSpec((None, PAIR, n, dim), lambda h, i, c: (i, h, 0, 0))
    buf = pltpu.VMEM((heads, BUF_KEYS, dim), jnp.bfloat16)
    stat = pltpu.VMEM((PAIR, rows, dim), jnp.float32)
    state = jax.ShapeDtypeStruct(q_t.shape, jnp.float32)
    return pl.pallas_call(
        shared_kernel,
        grid_spec=pltpu.PrefetchScalarGridSpec(
            num_scalar_prefetch=1,
            grid=(heads // PAIR, count),
            in_specs=[part(rows), part(chunk), part(chunk), pl.BlockSpec(memory_space=pl.ANY)],
            out_specs=[part(rows), part(rows)],
            scratch_shapes=[buf, buf, stat, stat, pltpu.SemaphoreType.DMA((2,))],
        ),
        out_shape=[state, state],
        compiler_params=pltpu.CompilerParams(vmem_limit_bytes=48 * 2 ** 20),
        cost_estimate=pl.CostEstimate(
            flops=6 * q_t.size * 1152, bytes_accessed=40 * 2 ** 20, transcendentals=q_t.size * 9),
        name='attend_shared',
    )(codes, q_t, kn_t, vn_t, source)


def attend_window(first, count, codes, q_t, acc, stats, source, old):
    total, heads, rows, dim = q_t.shape
    part = pl.BlockSpec((None, PAIR, rows, dim), lambda i, h, c: (first + i, h, 0, 0))
    anywhere = pl.BlockSpec(memory_space=pl.ANY)
    buf = pltpu.VMEM((heads, BUF_KEYS, dim), jnp.bfloat16)
    stat = pltpu.VMEM((PAIR, rows, dim), jnp.float32)
    specs, operands, alias = [part, part, part, anywhere], [q_t, acc, stats, source], {}
    body = window_kernel
    if old is None:
        inner = body
        body = lambda c, q, a, s, src, *rest: inner(c, q, a, s, src, None, *rest)
    else:
        specs, operands, alias = specs + [anywhere], operands + [old], {5: 0}
    return pl.pallas_call(
        body,
        grid_spec=pltpu.PrefetchScalarGridSpec(
            num_scalar_prefetch=1,
            grid=(count, heads // PAIR),
            in_specs=specs,
            out_specs=pl.BlockSpec((None, heads * rows, dim), lambda i, h, c: (first + i, 0, 0)),
            scratch_shapes=[buf, buf, stat, stat, pltpu.VMEM((PAIR, rows, dim), jnp.float32),
                            pltpu.VMEM((heads * rows, dim), jnp.float32), pltpu.SemaphoreType.DMA((2,))],
        ),
        out_shape=jax.ShapeDtypeStruct((total, heads * rows, dim), jnp.bfloat16),
        input_output_aliases=alias,
        compiler_params=pltpu.CompilerParams(vmem_limit_bytes=48 * 2 ** 20),
        cost_estimate=pl.CostEstimate(
            flops=6 * count * heads * rows * dim * 1024, bytes_accessed=count * 12 * 2 ** 20,
            transcendentals=count * heads * rows * 1024),
        name='attend_window',
    )(codes.reshape(-1), *operands)


def listing(codes, keep):
    keep_i = keep.astype(jnp.int32)
    n = codes.shape[1]
    place = jnp.sum(jnp.where(jnp.arange(n)[:, None] > jnp.arange(n), keep_i[:, None, :], 0), axis=2)
    pick = keep[:, None, :] & (place[:, None, :] == jnp.arange(n + LIST_PAD - 1)[:, None])
    packed = jnp.sum(jnp.where(pick, codes[:, None, :], 0), axis=2)
    return jnp.concatenate([jnp.sum(keep_i, axis=1, keepdims=True), packed], axis=1)


def spread(blocks, n_dev):
    chips = n_dev // CORES
    groups = [list(range(core, n_dev, CORES)) for core in range(CORES)]
    copies = jnp.broadcast_to(blocks[None], (chips,) + blocks.shape).reshape((-1,) + blocks.shape[1:])
    got = lax.all_to_all(copies, 'pool', 0, 0, axis_index_groups=groups, tiled=True)
    return got, lax.ppermute(got, 'pool', [(i, i ^ 1) for i in range(n_dev)])


def spread_place(device, slot, me):
    chips_first = (device // CORES) * SHARED_CAP + slot
    return chips_first + jnp.where(device % CORES == me % CORES, 0, N_CHIPS * SHARED_CAP)


def tri(n, strict=True):
    a, b = jnp.arange(n)[:, None], jnp.arange(n)[None, :]
    return (a < b if strict else a <= b).astype(jnp.float32)


def solution(mesh):
    n_dev = mesh.shape['pool']

    def local_step(queries, k_new, v_new, k_pool, v_pool, block_table, write_ids):
        req_count, chunk_len, q_heads, head_dim = queries.shape
        kv_heads = k_new.shape[2]
        per_dev, block_len = k_pool.shape[:2]
        n_pref = block_table.shape[1]
        groups = q_heads // kv_heads
        me = lax.axis_index('pool')

        tab = block_table.reshape(n_dev, req_count, n_pref)
        owners = block_table // per_dev
        local_ids = block_table % per_dev
        first = tab[:, 0]
        in_all = (first[:, None, :, None] == tab[:, 1:, None, :]).any(-1).all(1)
        shared = ((tab[..., None] == first[:, None, None, :]) & in_all[:, None, None, :]).any(-1)
        shared = shared.reshape(n_dev * req_count, n_pref)

        lanes = 128
        n_hi = n_dev * per_dev // lanes
        flat_first, flat_in = first.reshape(-1), in_all.reshape(-1)
        hot_hi = ((flat_first // lanes)[:, None] == jnp.arange(n_hi)) & flat_in[:, None]
        hot_lo = (flat_first % lanes)[:, None] == jnp.arange(lanes)
        named = jnp.einsum('eh,el->hl', hot_hi.astype(jnp.bfloat16), hot_lo.astype(jnp.bfloat16),
                           preferred_element_type=jnp.float32) > 0
        named_f = named.astype(jnp.float32)
        before = named_f @ tri(lanes)
        hi_count = jnp.sum(named_f, axis=1)
        hi_before = hi_count @ tri(n_hi)
        rank = (before + hi_before[:, None]).astype(jnp.int32)
        owner_count = jnp.sum(hi_count.reshape(n_dev, -1), axis=1).astype(jnp.int32)
        owner_base = hi_before[::n_hi // n_dev].astype(jnp.int32)

        win_count = jnp.sum((owners[:, :, None] == jnp.arange(n_dev)) & ~shared[:, :, None], axis=1)
        fits = (jnp.max(win_count) <= FAST_CAP) & (jnp.max(owner_count) <= RELAY_CAP * n_dev)
        fits = fits & (jnp.sum(owner_count) <= SHARED_CAP * n_dev)

        k_flat = k_pool.reshape(per_dev, block_len * kv_heads, head_dim)
        v_flat = v_pool.reshape(per_dev, block_len * kv_heads, head_dim)
        gather = lambda ids: gather_blocks(ids, k_flat, v_flat, kv_heads, block_len)
        exchange = lambda x: lax.all_to_all(x, 'pool', 0, 0, tiled=True)

        def slots(is_window, cap):
            mine = (owners == me) & is_window
            place = (mine.astype(jnp.float32) @ tri(n_pref)).astype(jnp.int32)
            pick = mine[:, None, :] & (place[:, None, :] == jnp.arange(cap)[:, None])
            send = jnp.sum(jnp.where(pick, local_ids[:, None, :], 0), axis=2)
            rows = lambda x: lax.dynamic_slice_in_dim(x, me * req_count, req_count, 0)
            own, win = rows(owners), rows(is_window)
            earlier = (own[:, :, None] == own[:, None, :]) & win[:, None, :] & (tri(n_pref).T > 0)
            code = own * cap + jnp.sum(earlier, axis=2)
            return send.reshape(n_dev, req_count, cap), code

        def prepare():
            q_t = queries.reshape(req_count, chunk_len, kv_heads, groups, head_dim).transpose(0, 2, 3, 1, 4)
            q_t = q_t.reshape(req_count, kv_heads, groups * chunk_len, head_dim)
            stored = store_chunk(write_ids, k_new, v_new, k_flat, v_flat)
            return (q_t, k_new.transpose(0, 2, 1, 3), v_new.transpose(0, 2, 1, 3)), stored

        my_base = lax.dynamic_index_in_dim(owner_base, me, keepdims=False)
        j = jnp.arange(n_dev)[:, None]
        want = my_base + jnp.arange(RELAY_CAP) * n_dev + (j - my_base) % n_dev
        mine = per_dev // lanes
        my_named = lax.dynamic_slice_in_dim(named, me * mine, mine, 0).reshape(-1)
        my_rank = lax.dynamic_slice_in_dim(rank, me * mine, mine, 0).reshape(-1)
        pick = my_named & (my_rank == want.reshape(-1)[:, None])
        relay_ids = jnp.sum(jnp.where(pick, jnp.arange(per_dev), 0), axis=1)
        relayed = exchange(gather(relay_ids))
        send, code = slots(~shared, FAST_CAP)
        early = gather(send[:, :EARLY].reshape(-1))
        relayed, early = lax.optimization_barrier((relayed, early))

        def fast():
            t_rank = jnp.arange(SHARED_CAP) * n_dev + me
            owner_end = owner_base + owner_count
            t_owner = jnp.minimum(jnp.sum(owner_end[None, :] <= t_rank[:, None], axis=1), n_dev - 1)
            t_base = jnp.sum(jnp.where(t_owner[:, None] == jnp.arange(n_dev), owner_base, 0), axis=1)
            t_slot = jnp.clip((t_rank - t_base) // n_dev, 0, RELAY_CAP - 1)
            near, far = spread(relayed[t_owner * RELAY_CAP + t_slot], n_dev)
            chunk, stored = prepare()
            late = gather(send[:, EARLY:].reshape(-1))
            ready, near, chunk, late = lax.optimization_barrier((early, near, chunk, late))
            shared_blocks = jnp.concatenate([near, far])
            my_shared = lax.dynamic_slice_in_dim(shared, me * req_count, req_count, 0)
            my_tab = lax.dynamic_slice_in_dim(block_table, me * req_count, 1, 0).reshape(-1)
            my_hi = ((my_tab // lanes)[:, None] == jnp.arange(n_hi)).astype(jnp.float32)
            my_lo = (my_tab % lanes)[:, None] == jnp.arange(lanes)
            my_rank_of = jnp.sum(jnp.where(my_lo, my_hi @ jnp.minimum(rank, 255).astype(jnp.float32), 0), axis=1)
            my_rank_of = my_rank_of.astype(jnp.int32)
            shared_code = spread_place(my_rank_of % n_dev, my_rank_of // n_dev, me)
            shared_list = listing(shared_code[None], my_shared[:1])
            own, slot = code // FAST_CAP, code % FAST_CAP
            place = lambda r, n: own[r] * (n * FAST_CAP) + slot[r]
            early_code = jnp.stack([place(r, EARLY) + r * FAST_CAP for r in range(EARLY)])
            n_late = req_count - EARLY
            late_code = jnp.stack([place(EARLY + r, n_late) + r * FAST_CAP for r in range(n_late)])
            early_list, late_list = listing(early_code, ~my_shared[:EARLY]), listing(late_code, ~my_shared[EARLY:])

            early_win = exchange(ready)
            acc, stats = attend_shared(shared_list.reshape(-1), *chunk, shared_blocks)
            late, acc, stats, stored = lax.optimization_barrier((late, acc, stats, stored))
            late_win = exchange(late)
            attn = attend_window(0, EARLY, early_list, chunk[0], acc, stats, early_win, None)
            attn = attend_window(EARLY, n_late, late_list, chunk[0], acc, stats, late_win, attn)
            return attn, *stored

        def full():
            send, codes = slots(jnp.ones_like(shared), FULL_CAP)
            blocks = exchange(gather(send.reshape(-1)))
            places = codes // FULL_CAP * (req_count * FULL_CAP) + codes % FULL_CAP
            places += jnp.arange(req_count)[:, None] * FULL_CAP
            chunk, stored = prepare()
            none = jnp.zeros((n_pref + LIST_PAD,), jnp.int32)
            acc, stats = attend_shared(none, *chunk, blocks)
            lists = listing(places, jnp.ones_like(places, dtype=bool))
            return attend_window(0, req_count, lists, chunk[0], acc, stats, blocks, None), *stored

        attn, k_out, v_out = lax.cond(fits, fast, full)
        return attn.reshape(queries.shape), k_out.reshape(k_pool.shape), v_out.reshape(v_pool.shape)

    row_spec = P('pool')
    return jax.shard_map(local_step, mesh=mesh, in_specs=(row_spec, row_spec, row_spec, row_spec, row_spec, P(), row_spec), out_specs=(row_spec, row_spec, row_spec), check_vma=False)
```

profile of v0, /device:TPU:11, one launch (start us, length us, event | category | flops | bytes accessed | tf_op | source)
XLA Modules:
  0.0 348.5 jit_solution(16887827428438001781)
XLA Ops:
  0.6 0.8 slice.55
  1.4 0.8 slice.56
  2.2 1.3 compare_reduce_fusion
  3.5 1.4 convert_reduce_fusion.5
  6.7 1.4 convert_reduce_fusion.6
  9.0 0.7 select_reduce_fusion.11.ids_ref
  9.7 5.7 %gather_blocks.6 = bf16[32,2,8,16,128]{4,3,2,1,0:T(8,128)(2,1)} custom-call(s32[32]{0:T(128)} %select_reduce_fusion.11.ids_ref, bf16[512,128,128]{2,1,0:T(8,128)(2,1)} %bitcast.111, bf16[512,128,128]{2,1,0:T(8,128)(2,1)} %bitcast.115), custom_call_target="tpu_custom_call" | custom-call | flops 256000000 | bytes 4194304 | tf_op jit(solution)/shard_map/gather_blocks/pallas_call | solution.py:61
  15.4 3.5 all-to-all-start.4
  18.9 2.6 and_reduce_fusion
  23.2 1.2 convert_reduce_fusion.4
  27.0 19.8 %gather_blocks.7 = bf16[192,2,8,16,128]{4,3,2,1,0:T(8,128)(2,1)} custom-call(s32[192]{0:T(256)} %reshape.749.ids_ref, bf16[512,128,128]{2,1,0:T(8,128)(2,1)} %bitcast.112, bf16[512,128,128]{2,1,0:T(8,128)(2,1)} %bitcast.116), custom_call_target="tpu_custom_call" | custom-call | flops 1536000000 | bytes 25165824 | tf_op jit(solution)/shard_map/gather_blocks/pallas_call | solution.py:61
  47.4 300.8 %conditional.1 = (bf16[512,128,128]{2,1,0:T(8,128)(2,1)}, bf16[512,128,128]{2,1,0:T(8,128)(2,1)}, bf16[4,128,40,128]{3,2,1,0:T(8,128)(2,1)}) conditional(s32[]{:T(128)} %convert_element_type.82, (s32[4,8]{1,0:T(4,128)S(1)}, bf16[4,128,8,128]{3,2,1,0:T(8,128)(2,1)}, bf16[4,128,8,128]{3,2,1,0:T(8,128)(2,1)}, bf16[512,128,128]{2,1,0:T(8,128)(2,1)}, ...), branch_computations={%region_11.17_spmd, %region_17.32_spmd} | conditional | flops 54468927488 | bytes 609476736 | solution.py:424
  49.0 3.1 broadcast_in_dim.150
  52.1 4.7 %all-to-all-start = ((bf16[64,2,8,16,128]{4,3,2,1,0:T(8,128)(2,1)}), bf16[64,2,8,16,128]{4,3,2,1,0:T(8,128)(2,1)}, u32[]{:S(2)}, u32[]{:S(2)}) async-start(bf16[64,2,8,16,128]{4,3,2,1,0:T(8,128)(2,1)} %bitcast.119), calls=%async_computation | async-start | bytes 8388608 | tf_op jit(solution)/shard_map/cond/branch_1_fun/all_to_all | solution.py:292
  57.6 6.2 %copy.64 = bf16[4,128,40,128]{3,1,2,0:T(8,128)(2,1)} copy(bf16[4,128,40,128]{3,2,1,0:T(8,128)(2,1)} %get-tuple-element.208) | data formatting | bytes 10485760 | tf_op jit(solution)/shard_map
  63.8 8.1 %gather_blocks.5 = bf16[64,2,8,16,128]{4,3,2,1,0:T(8,128)(2,1)} custom-call(s32[64]{0:T(128)} %reshape.730.ids_ref, bf16[512,128,128]{2,1,0:T(8,128)(2,1)} %get-tuple-element.81.k_hbm.k_ref, bf16[512,128,128]{2,1,0:T(8,128)(2,1)} %get-tuple-element.82.v_hbm.v_ref), custom_call_target="tpu_custom_call" | custom-call | flops 512000000 | bytes 8388608 | tf_op jit(solution)/shard_map/cond/branch_1_fun/gather_blocks/pallas_call | solution.py:61
  72.0 1.8 copy_bitcast_fusion.2
  73.7 36.6 %all-to-all-done = bf16[64,2,8,16,128]{4,3,2,1,0:T(8,128)(2,1)} async-done(((bf16[64,2,8,16,128]{4,3,2,1,0:T(8,128)(2,1)}), bf16[64,2,8,16,128]{4,3,2,1,0:T(8,128)(2,1)}, u32[]{:S(2)}, u32[]{:S(2)}) %all-to-all-start) | async-done | bytes 4194336 | tf_op jit(solution)/shard_map/cond/branch_1_fun/all_to_all | solution.py:292
  110.3 5.2 %all-to-all-start.2 = ((bf16[192,2,8,16,128]{4,3,2,1,0:T(8,128)(2,1)}), bf16[192,2,8,16,128]{4,3,2,1,0:T(8,128)(2,1)}, u32[]{:S(2)}, u32[]{:S(2)}) async-start(bf16[192,2,8,16,128]{4,3,2,1,0:T(8,128)(2,1)} %get-tuple-element.103), calls=%async_computation.2 | async-start | bytes 25165824 | tf_op jit(solution)/shard_map/cond/branch_1_fun/all_to_all | solution.py:347
  118.4 0.7 and_select_fusion.6
  119.5 4.9 %fusion.6 = (s32[135]{0:T(256)S(1)}, s32[135]{0:T(256)S(1)}) fusion(pred[128]{0:T(512)(128)(4,1)S(1)} %get-tuple-element.240, s32[128]{0:T(128)S(1)} %get-tuple-element.234, s32[128]{0:T(128)S(1)} %select_reduce_fusion.6, s32[128]{0:T(128)S(1)} %fusion.13, s32[128]{0:T(128)S(1)} %select_reduce_fusion.8, pred[128]{0:T(512)(128)(4,1)S(1)} %get-tuple-element.242), kind=kLoop, calls=%fused_computation.41 | loop fusion | flops 137970 | bytes 3384 | tf_op jit(solution)/shard_map/cond/branch_1_fun/reduce_sum | solution.py:284
  124.4 0.7 pad_add_fusion.2
  125.8 36.9 %store_chunk.3 = (bf16[512,128,128]{2,1,0:T(8,128)(2,1)}, bf16[512,128,128]{2,1,0:T(8,128)(2,1)}) custom-call(s32[512]{0:T(512)} %broadcast_add_fusion.1.from_ref, bf16[32,128,128]{2,1,0:T(8,128)(2,1)S(1)} %bitcast.121, bf16[32,128,128]{2,1,0:T(8,128)(2,1)} %bitcast.123, bf16[512,128,128]{2,1,0:T(8,128)(2,1)} %get-tuple-element.81.k_hbm.k_ref, ...), custom_call_target="tpu_custom_call" | custom-call | flops 10000000000 | bytes 67108864 | tf_op jit(solution)/shard_map/cond/branch_1_fun/store_chunk/pallas_call | solution.py:103
  162.7 7.4 %pad_maximum_fusion.src_hbm = bf16[128,2,8,16,128]{4,3,2,1,0:T(8,128)(2,1)} fusion(bf16[64,2,8,16,128]{4,3,2,1,0:T(8,128)(2,1)} %collective-permute-done, bf16[64,2,8,16,128]{4,3,2,1,0:T(8,128)(2,1)} %all-to-all-done), kind=kLoop, calls=%fused_computation.30 | loop fusion | flops 4194304 | bytes 16777216 | tf_op jit(solution)/shard_map/cond/branch_1_fun/concatenate | solution.py:389
  170.1 55.5 %attend_shared.3 = (f32[4,8,640,128]{3,2,1,0:T(8,128)}, f32[4,8,640,128]{3,2,1,0:T(8,128)}) custom-call(s32[136]{0:T(256)S(1)} %bitcast.110, bf16[4,8,640,128]{3,2,1,0:T(8,128)(2,1)} %bitcast.106, bf16[4,8,128,128]{3,2,1,0:T(8,128)(2,1)S(1)} %get-tuple-element.88.kn_ref, bf16[4,8,128,128]{3,2,1,0:T(8,128)(2,1)S(1)} %get-tuple-element.89.vn_ref, ...), custom_call_target="tpu_custom_call" | custom-call | flops 18119393280 | bytes 41943040 | tf_op jit(solution)/shard_map/cond/branch_1_fun/attend_shared/pallas_call | solution.py:229
  225.6 47.2 %all-to-all-done.2.src = bf16[192,2,8,16,128]{4,3,2,1,0:T(8,128)(2,1)} async-done(((bf16[192,2,8,16,128]{4,3,2,1,0:T(8,128)(2,1)}), bf16[192,2,8,16,128]{4,3,2,1,0:T(8,128)(2,1)}, u32[]{:S(2)}, u32[]{:S(2)}) %all-to-all-start.2) | async-done | bytes 12582944 | tf_op jit(solution)/shard_map/cond/branch_1_fun/all_to_all | solution.py:347
  272.8 3.4 all-to-all-start.1
  277.0 0.7 pad_add_fusion.3
  277.7 2.5 copy-done
  280.2 47.1 %attend_window.4.old_ref = bf16[4,5120,128]{2,1,0:T(8,128)(2,1)} custom-call(s32[408]{0:T(512)S(1)} %reshape.736.c, bf16[4,8,640,128]{3,2,1,0:T(8,128)(2,1)S(1)} %bitcast.108, f32[4,8,640,128]{3,2,1,0:T(8,128)} %get-tuple-element.100.a.acc_in, f32[4,8,640,128]{3,2,1,0:T(8,128)} %get-tuple-element.101.s.stat_in, bf16[192,2,8,16,128]{4,3,2,1,0:T(8,128)(2,1)} %all-to-all-done.2.src), custom_call_target="tpu_custom_call" | custom-call | flops 12079595520 | bytes 37748736 | tf_op jit(solution)/shard_map/cond/branch_1_fun/attend_window/pallas_call | solution.py:259
  327.3 3.5 all-to-all-done.1.src_hbm
  330.8 17.2 %attend_window.5 = bf16[4,5120,128]{2,1,0:T(8,128)(2,1)} custom-call(s32[136]{0:T(256)S(1)} %bitcast.109, bf16[4,8,640,128]{3,2,1,0:T(8,128)(2,1)} %bitcast.107, f32[4,8,640,128]{3,2,1,0:T(8,128)} %get-tuple-element.100.a.acc_in, f32[4,8,640,128]{3,2,1,0:T(8,128)} %get-tuple-element.101.s.stat_in, ...), custom_call_target="tpu_custom_call", output_to_operand_aliasing={{}: (5, {})} | custom-call | flops 4026531840 | bytes 12582912 | tf_op jit(solution)/shard_map/cond/branch_1_fun/attend_window/pallas_call | solution.py:259
  (92 shorter events, 12.4 us)
Async XLA Ops:
  5.3 1.3 copy-start.12
  8.3 0.7 copy-start.10
  9.7 9.2 %copy-start.2 = (s32[64,128]{1,0:T(8,128)S(1)}, s32[64,128]{1,0:T(8,128)}, u32[]{:S(2)}) copy-start(s32[64,128]{1,0:T(8,128)} %param.14) | copy-start | bytes 98308
  15.4 32.0 %all-to-all-start.4 = ((bf16[32,2,8,16,128]{4,3,2,1,0:T(8,128)(2,1)}), bf16[32,2,8,16,128]{4,3,2,1,0:T(8,128)(2,1)S(1)}, u32[]{:S(2)}, u32[]{:S(2)}) async-start(bf16[32,2,8,16,128]{4,3,2,1,0:T(8,128)(2,1)} %gather_blocks.6), calls=%async_computation.4 | async-start | bytes 4194304 | tf_op jit(solution)/shard_map/all_to_all | solution.py:347
  21.4 0.6 copy-start.8
  27.0 20.5 %copy-start.9 = (s32[4,8]{1,0:T(4,128)S(1)}, s32[4,8]{1,0:T(4,128)}, u32[]{:S(2)}) copy-start(s32[4,8]{1,0:T(4,128)} %param.15) | copy-start | bytes 388
  27.0 20.5 %copy-start.11 = (s32[64,128]{1,0:T(8,128)S(1)}, s32[64,128]{1,0:T(8,128)}, u32[]{:S(2)}) copy-start(s32[64,128]{1,0:T(8,128)} %copy-done.10) | copy-start | bytes 98308
  27.0 20.4 %copy-start.13 = (s32[16]{0:T(128)S(1)}, s32[16]{0:T(128)}, u32[]{:S(2)}) copy-start(s32[16]{0:T(128)} %copy-done.12) | copy-start | bytes 196
  47.7 0.6 copy-start.3
  47.7 0.6 copy-start.4
  47.7 0.6 copy-start.6
  52.1 4.7 %copy-start.5 = (s32[16,4,4]{1,0,2:T(8,128)S(1)}, s32[16,4,4]{1,0,2:T(8,128)}, u32[]{:S(2)}) copy-start(s32[16,4,4]{1,0,2:T(8,128)} %copy-done.4) | copy-start | bytes 3076 | tf_op jit(solution)/shard_map/cond
  52.1 58.2 %all-to-all-start = ((bf16[64,2,8,16,128]{4,3,2,1,0:T(8,128)(2,1)}), bf16[64,2,8,16,128]{4,3,2,1,0:T(8,128)(2,1)}, u32[]{:S(2)}, u32[]{:S(2)}) async-start(bf16[64,2,8,16,128]{4,3,2,1,0:T(8,128)(2,1)} %bitcast.119), calls=%async_computation | async-start | bytes 8388608 | tf_op jit(solution)/shard_map/cond/branch_1_fun/all_to_all | solution.py:292
  63.8 8.2 %copy-start.1 = (bf16[4,128,8,128]{3,2,1,0:T(8,128)(2,1)S(1)}, bf16[4,128,8,128]{3,2,1,0:T(8,128)(2,1)}, u32[]{:S(2)}) copy-start(bf16[4,128,8,128]{3,2,1,0:T(8,128)(2,1)} %get-tuple-element.209) | copy-start | bytes 3145732 | tf_op jit(solution)/shard_map/cond
  110.3 9.1 %copy-start.7 = (s32[4,128]{1,0:T(4,128)S(1)}, s32[4,128]{1,0:T(4,128)}, u32[]{:S(2)}) copy-start(s32[4,128]{1,0:T(4,128)} %copy-done.6) | copy-start | bytes 6148 | tf_op jit(solution)/shard_map/cond
  110.3 162.5 %all-to-all-start.2 = ((bf16[192,2,8,16,128]{4,3,2,1,0:T(8,128)(2,1)}), bf16[192,2,8,16,128]{4,3,2,1,0:T(8,128)(2,1)}, u32[]{:S(2)}, u32[]{:S(2)}) async-start(bf16[192,2,8,16,128]{4,3,2,1,0:T(8,128)(2,1)} %get-tuple-element.103), calls=%async_computation.2 | async-start | bytes 25165824 | tf_op jit(solution)/shard_map/cond/branch_1_fun/all_to_all | solution.py:347
  115.5 47.2 %collective-permute-start = (bf16[64,2,8,16,128]{4,3,2,1,0:T(8,128)(2,1)}, bf16[64,2,8,16,128]{4,3,2,1,0:T(8,128)(2,1)}, u32[]{:S(2)}, u32[]{:S(2)}) collective-permute-start(bf16[64,2,8,16,128]{4,3,2,1,0:T(8,128)(2,1)} %all-to-all-done), channel_id=1, source_target_pairs={{0,1},{1,0},{2,3},{3,2},{4,5},{5,4},{6,7},{7,6},{8,9},{9,8},{10,11... | collective-permute-start | bytes 12582920 | tf_op jit(solution)/shard_map/cond/branch_1_fun/ppermute | solution.py:293
  272.8 57.9 %all-to-all-start.1 = ((bf16[64,2,8,16,128]{4,3,2,1,0:T(8,128)(2,1)}), bf16[64,2,8,16,128]{4,3,2,1,0:T(8,128)(2,1)}, u32[]{:S(2)}, u32[]{:S(2)}) async-start(bf16[64,2,8,16,128]{4,3,2,1,0:T(8,128)(2,1)} %gather_blocks.5), calls=%async_computation.1 | async-start | bytes 8388608 | tf_op jit(solution)/shard_map/cond/branch_1_fun/all_to_all | solution.py:347
  277.7 2.5 copy-start
where the time goes:
time: 355 us; the launch traced here: 348 us
  Pallas kernels  190 us (54%)
  waiting for transfers between devices  87.7 us (25%)
  other arithmetic  26.9 us (8%)
  local copies, waits for them, and re-layouts  20.7 us (6%)
  starting transfers between devices  17.1 us (5%)
    pallas_call x2, Pallas kernels, attend_window(): pl.pallas_call(body, grid_spec=pltpu.PrefetchScalarGridSpec(num_scalar_pr...  64.2 us
    pallas_call x1, Pallas kernels, attend_shared(): pl.pallas_call(shared_kernel, grid_spec=pltpu.PrefetchScalarGridSpec(num_...  55.5 us
    all_to_all x3, waiting for transfers between devices, local_step(): exchange = lambda x: lax.all_to_all(x, 'pool', 0, 0, tiled=True)  51.1 us
    pallas_call x1, Pallas kernels, store_chunk(): pl.pallas_call(store_kernel, grid_spec=pltpu.PrefetchScalarGridSpec(num_s...  36.9 us
    all_to_all x1, waiting for transfers between devices, spread(): lax.all_to_all(copies, 'pool', 0, 0, axis_index_groups=groups, tiled=True)  36.6 us
    pallas_call x3, Pallas kernels, gather_blocks(): pl.pallas_call(gather_kernel, grid_spec=pltpu.PrefetchScalarGridSpec(num_...  33.7 us
    all_to_all x3, starting transfers between devices, local_step(): exchange = lambda x: lax.all_to_all(x, 'pool', 0, 0, tiled=True)  12 us
    concatenate x1, other arithmetic, fast(): shared_blocks = jnp.concatenate([near, far])  7.38 us
  transfers between devices with their start and end apart: 5, of which 4 were waited for; matrix products, arithmetic and copies ran while one was open for 10% of the time, Pallas kernels for 48%

commit v1 on v0

--- a/solution.py
+++ b/solution.py
@@ -11,7 +11,7 @@
 FULL_CAP = 20
 RELAY_CAP = 2
 SHARED_CAP = 8
-GROUP = 8
+GROUP = 16
 STORE_BLOCKS = 16
 GROUP_HEADS = 5
 PAIR = 2

time: 355 us -> 352 us (level)
  Pallas kernels: 190 us -> 182 us
  waiting for transfers between devices: 87.7 us -> 93.5 us
    pallas_call x3, Pallas kernels: 33.7 us -> 25.7 us  [gather_blocks(): pl.pallas_call(gather_kernel, grid_spec=pltpu.PrefetchScalarGridSpec(num_...]
    all_to_all x3, waiting for transfers between devices: 51.1 us -> 55.5 us  [local_step(): exchange = lambda x: lax.all_to_all(x, 'pool', 0, 0, tiled=True)]
  transfers between devices with their start and end apart: 5 -> 5, of which waited for: 4 -> 4; matrix products, arithmetic and copies ran while one was open for 10% -> 10% of each run, Pallas kernels for 48% -> 46%
where the time goes in v1:
time: 352 us; the launch traced here: 349 us
  Pallas kernels  182 us (52%)
  waiting for transfers between devices  93.5 us (27%)
  other arithmetic  26.9 us (8%)
  local copies, waits for them, and re-layouts  20.7 us (6%)
  starting transfers between devices  19.4 us (6%)
    pallas_call x2, Pallas kernels, attend_window(): pl.pallas_call(body, grid_spec=pltpu.PrefetchScalarGridSpec(num_scalar_pr...  64.2 us
    pallas_call x1, Pallas kernels, attend_shared(): pl.pallas_call(shared_kernel, grid_spec=pltpu.PrefetchScalarGridSpec(num_...  55.5 us
    all_to_all x3, waiting for transfers between devices, local_step(): exchange = lambda x: lax.all_to_all(x, 'pool', 0, 0, tiled=True)  55.5 us
    all_to_all x1, waiting for transfers between devices, spread(): lax.all_to_all(copies, 'pool', 0, 0, axis_index_groups=groups, tiled=True)  37.9 us
    pallas_call x1, Pallas kernels, store_chunk(): pl.pallas_call(store_kernel, grid_spec=pltpu.PrefetchScalarGridSpec(num_s...  36.9 us
    pallas_call x3, Pallas kernels, gather_blocks(): pl.pallas_call(gather_kernel, grid_spec=pltpu.PrefetchScalarGridSpec(num_...  25.7 us
    all_to_all x3, starting transfers between devices, local_step(): exchange = lambda x: lax.all_to_all(x, 'pool', 0, 0, tiled=True)  14.3 us
    concatenate x1, other arithmetic, fast(): shared_blocks = jnp.concatenate([near, far])  7.38 us
  transfers between devices with their start and end apart: 5, of which 4 were waited for; matrix products, arithmetic and copies ran while one was open for 10% of the time, Pallas kernels for 46%

profile of v1, /device:TPU:11, one launch (start us, length us, event | category | flops | bytes accessed | tf_op | source)
XLA Modules:
  0.0 348.5 jit_solution(9991466092384095451)
XLA Ops:
  0.6 0.8 slice.55
  1.4 0.8 slice.56
  2.2 1.3 compare_reduce_fusion
  3.5 1.4 convert_reduce_fusion.5
  6.7 1.4 convert_reduce_fusion.6
  9.7 3.8 %gather_blocks.6 = bf16[32,2,8,16,128]{4,3,2,1,0:T(8,128)(2,1)} custom-call(s32[32]{0:T(128)} %select_reduce_fusion.11.ids_ref, bf16[512,128,128]{2,1,0:T(8,128)(2,1)} %bitcast.111, bf16[512,128,128]{2,1,0:T(8,128)(2,1)} %bitcast.115), custom_call_target="tpu_custom_call" | custom-call | flops 256000000 | bytes 4194304 | tf_op jit(solution)/shard_map/gather_blocks/pallas_call | solution.py:61
  13.5 5.8 %all-to-all-start.4 = ((bf16[32,2,8,16,128]{4,3,2,1,0:T(8,128)(2,1)}), bf16[32,2,8,16,128]{4,3,2,1,0:T(8,128)(2,1)S(1)}, u32[]{:S(2)}, u32[]{:S(2)}) async-start(bf16[32,2,8,16,128]{4,3,2,1,0:T(8,128)(2,1)} %gather_blocks.6), calls=%async_computation.4 | async-start | bytes 4194304 | tf_op jit(solution)/shard_map/all_to_all | solution.py:347
  19.3 2.6 and_reduce_fusion
  23.7 1.2 convert_reduce_fusion.4
  27.5 15.5 %gather_blocks.7 = bf16[192,2,8,16,128]{4,3,2,1,0:T(8,128)(2,1)} custom-call(s32[192]{0:T(256)} %reshape.749.ids_ref, bf16[512,128,128]{2,1,0:T(8,128)(2,1)} %bitcast.112, bf16[512,128,128]{2,1,0:T(8,128)(2,1)} %bitcast.116), custom_call_target="tpu_custom_call" | custom-call | flops 1536000000 | bytes 25165824 | tf_op jit(solution)/shard_map/gather_blocks/pallas_call | solution.py:61
  43.1 4.8 %all-to-all-done.4 = bf16[32,2,8,16,128]{4,3,2,1,0:T(8,128)(2,1)S(1)} async-done(((bf16[32,2,8,16,128]{4,3,2,1,0:T(8,128)(2,1)}), bf16[32,2,8,16,128]{4,3,2,1,0:T(8,128)(2,1)S(1)}, u32[]{:S(2)}, u32[]{:S(2)}) %all-to-all-start.4) | async-done | bytes 2097184 | tf_op jit(solution)/shard_map/all_to_all | solution.py:347
  47.9 300.4 %conditional.1 = (bf16[512,128,128]{2,1,0:T(8,128)(2,1)}, bf16[512,128,128]{2,1,0:T(8,128)(2,1)}, bf16[4,128,40,128]{3,2,1,0:T(8,128)(2,1)}) conditional(s32[]{:T(128)} %convert_element_type.82, (s32[4,8]{1,0:T(4,128)S(1)}, bf16[4,128,8,128]{3,2,1,0:T(8,128)(2,1)}, bf16[4,128,8,128]{3,2,1,0:T(8,128)(2,1)}, bf16[512,128,128]{2,1,0:T(8,128)(2,1)}, ...), branch_computations={%region_11.17_spmd, %region_17.32_spmd} | conditional | flops 54468927488 | bytes 609476736 | solution.py:424
  49.4 3.1 broadcast_in_dim.150
  52.6 4.7 %all-to-all-start = ((bf16[64,2,8,16,128]{4,3,2,1,0:T(8,128)(2,1)}), bf16[64,2,8,16,128]{4,3,2,1,0:T(8,128)(2,1)}, u32[]{:S(2)}, u32[]{:S(2)}) async-start(bf16[64,2,8,16,128]{4,3,2,1,0:T(8,128)(2,1)} %bitcast.119), calls=%async_computation | async-start | bytes 8388608 | tf_op jit(solution)/shard_map/cond/branch_1_fun/all_to_all | solution.py:292
  58.0 6.2 %copy.64 = bf16[4,128,40,128]{3,1,2,0:T(8,128)(2,1)} copy(bf16[4,128,40,128]{3,2,1,0:T(8,128)(2,1)} %get-tuple-element.208) | data formatting | bytes 10485760 | tf_op jit(solution)/shard_map
  64.3 6.4 %gather_blocks.5 = bf16[64,2,8,16,128]{4,3,2,1,0:T(8,128)(2,1)} custom-call(s32[64]{0:T(128)} %reshape.730.ids_ref, bf16[512,128,128]{2,1,0:T(8,128)(2,1)} %get-tuple-element.81.k_hbm.k_ref, bf16[512,128,128]{2,1,0:T(8,128)(2,1)} %get-tuple-element.82.v_hbm.v_ref), custom_call_target="tpu_custom_call" | custom-call | flops 512000000 | bytes 8388608 | tf_op jit(solution)/shard_map/cond/branch_1_fun/gather_blocks/pallas_call | solution.py:61
  70.7 1.8 copy_bitcast_fusion.2
  72.5 37.9 %all-to-all-done = bf16[64,2,8,16,128]{4,3,2,1,0:T(8,128)(2,1)} async-done(((bf16[64,2,8,16,128]{4,3,2,1,0:T(8,128)(2,1)}), bf16[64,2,8,16,128]{4,3,2,1,0:T(8,128)(2,1)}, u32[]{:S(2)}, u32[]{:S(2)}) %all-to-all-start) | async-done | bytes 4194336 | tf_op jit(solution)/shard_map/cond/branch_1_fun/all_to_all | solution.py:292
  110.4 5.1 %all-to-all-start.2 = ((bf16[192,2,8,16,128]{4,3,2,1,0:T(8,128)(2,1)}), bf16[192,2,8,16,128]{4,3,2,1,0:T(8,128)(2,1)}, u32[]{:S(2)}, u32[]{:S(2)}) async-start(bf16[192,2,8,16,128]{4,3,2,1,0:T(8,128)(2,1)} %get-tuple-element.103), calls=%async_computation.2 | async-start | bytes 25165824 | tf_op jit(solution)/shard_map/cond/branch_1_fun/all_to_all | solution.py:347
  118.5 0.7 and_select_fusion.6
  119.5 4.9 %fusion.6 = (s32[135]{0:T(256)S(1)}, s32[135]{0:T(256)S(1)}) fusion(pred[128]{0:T(512)(128)(4,1)S(1)} %get-tuple-element.240, s32[128]{0:T(128)S(1)} %get-tuple-element.234, s32[128]{0:T(128)S(1)} %select_reduce_fusion.6, s32[128]{0:T(128)S(1)} %fusion.13, s32[128]{0:T(128)S(1)} %select_reduce_fusion.8, pred[128]{0:T(512)(128)(4,1)S(1)} %get-tuple-element.242), kind=kLoop, calls=%fused_computation.41 | loop fusion | flops 137970 | bytes 3384 | tf_op jit(solution)/shard_map/cond/branch_1_fun/reduce_sum | solution.py:284
  124.4 0.7 pad_add_fusion.2
  125.8 36.9 %store_chunk.3 = (bf16[512,128,128]{2,1,0:T(8,128)(2,1)}, bf16[512,128,128]{2,1,0:T(8,128)(2,1)}) custom-call(s32[512]{0:T(512)} %broadcast_add_fusion.1.from_ref, bf16[32,128,128]{2,1,0:T(8,128)(2,1)S(1)} %bitcast.121, bf16[32,128,128]{2,1,0:T(8,128)(2,1)} %bitcast.123, bf16[512,128,128]{2,1,0:T(8,128)(2,1)} %get-tuple-element.81.k_hbm.k_ref, ...), custom_call_target="tpu_custom_call" | custom-call | flops 10000000000 | bytes 67108864 | tf_op jit(solution)/shard_map/cond/branch_1_fun/store_chunk/pallas_call | solution.py:103
  162.7 7.4 %pad_maximum_fusion.src_hbm = bf16[128,2,8,16,128]{4,3,2,1,0:T(8,128)(2,1)} fusion(bf16[64,2,8,16,128]{4,3,2,1,0:T(8,128)(2,1)} %collective-permute-done, bf16[64,2,8,16,128]{4,3,2,1,0:T(8,128)(2,1)} %all-to-all-done), kind=kLoop, calls=%fused_computation.30 | loop fusion | flops 4194304 | bytes 16777216 | tf_op jit(solution)/shard_map/cond/branch_1_fun/concatenate | solution.py:389
  170.1 55.5 %attend_shared.3 = (f32[4,8,640,128]{3,2,1,0:T(8,128)}, f32[4,8,640,128]{3,2,1,0:T(8,128)}) custom-call(s32[136]{0:T(256)S(1)} %bitcast.110, bf16[4,8,640,128]{3,2,1,0:T(8,128)(2,1)} %bitcast.106, bf16[4,8,128,128]{3,2,1,0:T(8,128)(2,1)S(1)} %get-tuple-element.88.kn_ref, bf16[4,8,128,128]{3,2,1,0:T(8,128)(2,1)S(1)} %get-tuple-element.89.vn_ref, ...), custom_call_target="tpu_custom_call" | custom-call | flops 18119393280 | bytes 41943040 | tf_op jit(solution)/shard_map/cond/branch_1_fun/attend_shared/pallas_call | solution.py:229
  225.6 47.2 %all-to-all-done.2.src = bf16[192,2,8,16,128]{4,3,2,1,0:T(8,128)(2,1)} async-done(((bf16[192,2,8,16,128]{4,3,2,1,0:T(8,128)(2,1)}), bf16[192,2,8,16,128]{4,3,2,1,0:T(8,128)(2,1)}, u32[]{:S(2)}, u32[]{:S(2)}) %all-to-all-start.2) | async-done | bytes 12582944 | tf_op jit(solution)/shard_map/cond/branch_1_fun/all_to_all | solution.py:347
  272.9 3.4 all-to-all-start.1
  277.1 0.7 pad_add_fusion.3
  277.8 2.5 copy-done
  280.3 47.1 %attend_window.4.old_ref = bf16[4,5120,128]{2,1,0:T(8,128)(2,1)} custom-call(s32[408]{0:T(512)S(1)} %reshape.736.c, bf16[4,8,640,128]{3,2,1,0:T(8,128)(2,1)S(1)} %bitcast.108, f32[4,8,640,128]{3,2,1,0:T(8,128)} %get-tuple-element.100.a.acc_in, f32[4,8,640,128]{3,2,1,0:T(8,128)} %get-tuple-element.101.s.stat_in, bf16[192,2,8,16,128]{4,3,2,1,0:T(8,128)(2,1)} %all-to-all-done.2.src), custom_call_target="tpu_custom_call" | custom-call | flops 12079595520 | bytes 37748736 | tf_op jit(solution)/shard_map/cond/branch_1_fun/attend_window/pallas_call | solution.py:259
  327.4 3.5 all-to-all-done.1.src_hbm
  330.8 17.2 %attend_window.5 = bf16[4,5120,128]{2,1,0:T(8,128)(2,1)} custom-call(s32[136]{0:T(256)S(1)} %bitcast.109, bf16[4,8,640,128]{3,2,1,0:T(8,128)(2,1)} %bitcast.107, f32[4,8,640,128]{3,2,1,0:T(8,128)} %get-tuple-element.100.a.acc_in, f32[4,8,640,128]{3,2,1,0:T(8,128)} %get-tuple-element.101.s.stat_in, ...), custom_call_target="tpu_custom_call", output_to_operand_aliasing={{}: (5, {})} | custom-call | flops 4026531840 | bytes 12582912 | tf_op jit(solution)/shard_map/cond/branch_1_fun/attend_window/pallas_call | solution.py:259
  (92 shorter events, 12.7 us)
Async XLA Ops:
  5.3 1.3 copy-start.12
  8.3 0.7 copy-start.10
  9.7 9.7 %copy-start.2 = (s32[64,128]{1,0:T(8,128)S(1)}, s32[64,128]{1,0:T(8,128)}, u32[]{:S(2)}) copy-start(s32[64,128]{1,0:T(8,128)} %param.14) | copy-start | bytes 98308
  13.5 34.4 %all-to-all-start.4 = ((bf16[32,2,8,16,128]{4,3,2,1,0:T(8,128)(2,1)}), bf16[32,2,8,16,128]{4,3,2,1,0:T(8,128)(2,1)S(1)}, u32[]{:S(2)}, u32[]{:S(2)}) async-start(bf16[32,2,8,16,128]{4,3,2,1,0:T(8,128)(2,1)} %gather_blocks.6), calls=%async_computation.4 | async-start | bytes 4194304 | tf_op jit(solution)/shard_map/all_to_all | solution.py:347
  21.9 0.6 copy-start.8
  27.4 20.5 %copy-start.9 = (s32[4,8]{1,0:T(4,128)S(1)}, s32[4,8]{1,0:T(4,128)}, u32[]{:S(2)}) copy-start(s32[4,8]{1,0:T(4,128)} %param.15) | copy-start | bytes 388
  27.5 20.5 %copy-start.11 = (s32[64,128]{1,0:T(8,128)S(1)}, s32[64,128]{1,0:T(8,128)}, u32[]{:S(2)}) copy-start(s32[64,128]{1,0:T(8,128)} %copy-done.10) | copy-start | bytes 98308
  27.5 20.4 %copy-start.13 = (s32[16]{0:T(128)S(1)}, s32[16]{0:T(128)}, u32[]{:S(2)}) copy-start(s32[16]{0:T(128)} %copy-done.12) | copy-start | bytes 196
  48.2 0.6 copy-start.3
  48.2 0.6 copy-start.4
  48.2 0.6 copy-start.6
  52.6 4.7 %copy-start.5 = (s32[16,4,4]{1,0,2:T(8,128)S(1)}, s32[16,4,4]{1,0,2:T(8,128)}, u32[]{:S(2)}) copy-start(s32[16,4,4]{1,0,2:T(8,128)} %copy-done.4) | copy-start | bytes 3076 | tf_op jit(solution)/shard_map/cond
  52.6 57.9 %all-to-all-start = ((bf16[64,2,8,16,128]{4,3,2,1,0:T(8,128)(2,1)}), bf16[64,2,8,16,128]{4,3,2,1,0:T(8,128)(2,1)}, u32[]{:S(2)}, u32[]{:S(2)}) async-start(bf16[64,2,8,16,128]{4,3,2,1,0:T(8,128)(2,1)} %bitcast.119), calls=%async_computation | async-start | bytes 8388608 | tf_op jit(solution)/shard_map/cond/branch_1_fun/all_to_all | solution.py:292
  64.3 6.4 %copy-start.1 = (bf16[4,128,8,128]{3,2,1,0:T(8,128)(2,1)S(1)}, bf16[4,128,8,128]{3,2,1,0:T(8,128)(2,1)}, u32[]{:S(2)}) copy-start(bf16[4,128,8,128]{3,2,1,0:T(8,128)(2,1)} %get-tuple-element.209) | copy-start | bytes 3145732 | tf_op jit(solution)/shard_map/cond
  110.4 9.0 %copy-start.7 = (s32[4,128]{1,0:T(4,128)S(1)}, s32[4,128]{1,0:T(4,128)}, u32[]{:S(2)}) copy-start(s32[4,128]{1,0:T(4,128)} %copy-done.6) | copy-start | bytes 6148 | tf_op jit(solution)/shard_map/cond
  110.4 162.4 %all-to-all-start.2 = ((bf16[192,2,8,16,128]{4,3,2,1,0:T(8,128)(2,1)}), bf16[192,2,8,16,128]{4,3,2,1,0:T(8,128)(2,1)}, u32[]{:S(2)}, u32[]{:S(2)}) async-start(bf16[192,2,8,16,128]{4,3,2,1,0:T(8,128)(2,1)} %get-tuple-element.103), calls=%async_computation.2 | async-start | bytes 25165824 | tf_op jit(solution)/shard_map/cond/branch_1_fun/all_to_all | solution.py:347
  115.5 47.2 %collective-permute-start = (bf16[64,2,8,16,128]{4,3,2,1,0:T(8,128)(2,1)}, bf16[64,2,8,16,128]{4,3,2,1,0:T(8,128)(2,1)}, u32[]{:S(2)}, u32[]{:S(2)}) collective-permute-start(bf16[64,2,8,16,128]{4,3,2,1,0:T(8,128)(2,1)} %all-to-all-done), channel_id=1, source_target_pairs={{0,1},{1,0},{2,3},{3,2},{4,5},{5,4},{6,7},{7,6},{8,9},{9,8},{10,11... | collective-permute-start | bytes 12582920 | tf_op jit(solution)/shard_map/cond/branch_1_fun/ppermute | solution.py:293
  272.9 57.9 %all-to-all-start.1 = ((bf16[64,2,8,16,128]{4,3,2,1,0:T(8,128)(2,1)}), bf16[64,2,8,16,128]{4,3,2,1,0:T(8,128)(2,1)}, u32[]{:S(2)}, u32[]{:S(2)}) async-start(bf16[64,2,8,16,128]{4,3,2,1,0:T(8,128)(2,1)} %gather_blocks.5), calls=%async_computation.1 | async-start | bytes 8388608 | tf_op jit(solution)/shard_map/cond/branch_1_fun/all_to_all | solution.py:347
  277.8 2.5 copy-start
